TPU v7x, 16 devices: a 4x2x1 block of a 4x4x8 slice. The times are simulated.
16 devices in a mesh: dp: 2 (over y, z), ep: 8 (over x, core).
Axes of the slice: x: 4, y: 2, z: 1, core: 2. Of those that a mesh axis runs over, the one named last changes fastest.
The devices are a block of a 4x4x8 slice.
Arguments:
- h0: bfloat16 [16, 1024, 2048], P(('dp', 'ep')), parts along dimension 0
- idx: int32 [16, 1024, 6], P(('dp', 'ep')), parts along dimension 0
- slot: int32 [16, 1024, 6], P(('dp', 'ep')), parts along dimension 0
- norm_attn: bfloat16 [2048], replicated
- wq: bfloat16 [2048, 2048], replicated
- wk: bfloat16 [2048, 2048], replicated
- wv: bfloat16 [2048, 2048], replicated
- wo: bfloat16 [2048, 2048], replicated
- norm_ffn: bfloat16 [2048], replicated
- w1: bfloat16 [2048, 10944], replicated
- w3: bfloat16 [2048, 10944], replicated
- w2: bfloat16 [10944, 2048], replicated
- norm_moe: bfloat16 [2048], replicated
- wr: bfloat16 [2048, 64], replicated
- ue1: bfloat16 [64, 2048, 1408], P('ep')
- ue3: bfloat16 [64, 2048, 1408], P('ep')
- ue2: bfloat16 [64, 1408, 2048], P('ep')
Outputs:
- output: bfloat16 [16, 1024, 2048], P(('dp', 'ep')), parts along dimension 0
There are 2 independent parts. A program takes and returns all parts, laid end to end along the dimension named above; an argument that names none is the same for every part.
All inputs are finite; a program needn't handle non-finite values.
Results may differ from a plain program's by a relative error of at most 0.00946092.
Values are sent between devices in bfloat16 or wider.
A program may use at most 768 MiB of HBM per device.

v0:
```python
import jax
import jax.numpy as jnp
from jax import lax
from jax.sharding import PartitionSpec as P

HEAD = 128
EPS = 1e-6
ROPE_BASE = 10000.0


def _rms(x, w):
    xf = x.astype(jnp.float32)
    r = lax.rsqrt(jnp.mean(xf * xf, axis=-1, keepdims=True) + EPS)
    return (xf * r * w.astype(jnp.float32)).astype(jnp.bfloat16)


def _rope(x, cos, sin):
    h = HEAD // 2
    x1, x2 = x[..., :h], x[..., h:]
    return jnp.concatenate([x1 * cos - x2 * sin, x2 * cos + x1 * sin], axis=-1)


def _dense(h0, na, wq, wk, wv, wo, nf, w1, w3, w2):
    f32, bf = jnp.float32, jnp.bfloat16
    b, s, d = h0.shape
    nh = wq.shape[1] // HEAD
    nkvv = wk.shape[1] // HEAD
    pos = jnp.arange(s).astype(f32)
    inv = ROPE_BASE ** (-2.0 * jnp.arange(HEAD // 2).astype(f32) / HEAD)
    ang = pos[:, None] * inv[None, :]
    cos, sin = jnp.cos(ang)[:, None, :], jnp.sin(ang)[:, None, :]
    x = _rms(h0, na).reshape(b * s, d)
    q = _rope(jnp.dot(x, wq, preferred_element_type=f32).reshape(b, s, nh, HEAD), cos, sin).astype(bf)
    k = _rope(jnp.dot(x, wk, preferred_element_type=f32).reshape(b, s, nkvv, HEAD), cos, sin).astype(bf)
    v = jnp.dot(x, wv, preferred_element_type=f32).astype(bf).reshape(b, s, nkvv, HEAD)
    q = q.reshape(b, s, nkvv, nh // nkvv, HEAD)
    sc = jnp.einsum('bqgrd,bkgd->bgrqk', q, k, preferred_element_type=f32) * HEAD ** -0.5
    causal = jnp.arange(s)[:, None] >= jnp.arange(s)[None, :]
    sc = jnp.where(causal, sc, -jnp.inf)
    p = jax.nn.softmax(sc, axis=-1).astype(bf)
    o = jnp.einsum('bgrqk,bkgd->bqgrd', p, v, preferred_element_type=f32).astype(bf).reshape(b * s, nh * HEAD)
    a = (h0.reshape(b * s, d).astype(f32) + jnp.dot(o, wo, preferred_element_type=f32)).astype(bf)
    z = _rms(a, nf)
    hid = (jax.nn.silu(jnp.dot(z, w1, preferred_element_type=f32)) * jnp.dot(z, w3, preferred_element_type=f32)).astype(bf)
    return a.astype(f32) + jnp.dot(hid, w2, preferred_element_type=f32)


def _route(h0, nm, wr, idx):
    d = h0.shape[-1]
    k = idx.shape[-1]
    u = _rms(h0, nm).reshape(-1, d)
    logits = jnp.dot(u, wr, preferred_element_type=jnp.float32)
    g = jax.nn.softmax(jnp.take_along_axis(logits, idx.reshape(-1, k), axis=1), axis=-1)
    return u, g


def _experts(x, ue1, ue3, ue2):
    f32 = jnp.float32
    h1 = jnp.einsum('ecd,edf->ecf', x, ue1, preferred_element_type=f32)
    h3 = jnp.einsum('ecd,edf->ecf', x, ue3, preferred_element_type=f32)
    hid = (jax.nn.silu(h1) * h3).astype(jnp.bfloat16)
    return jnp.einsum('ecf,efd->ecd', hid, ue2, preferred_element_type=f32).astype(jnp.bfloat16)


def solution(mesh):
    G = mesh.shape['ep']

    def local(h0, idx, slot, na, wq, wk, wv, wo, nf, w1, w3, w2, nm, wr, ue1, ue3, ue2):
        f32 = jnp.float32
        b, s, d = h0.shape
        t = b * s
        k = idx.shape[-1]
        el = ue1.shape[0]
        e = el * G
        cap = 2 * t * k // e
        u, g = _route(h0, nm, wr, idx)
        ix = idx.reshape(t, k)
        sl = slot.reshape(t, k)
        rows = jnp.broadcast_to(jnp.arange(t, dtype=jnp.int32)[:, None], (t, k))
        tok = jnp.full((e, cap), t, jnp.int32).at[ix, sl].set(rows)
        send = jnp.take(u, tok, axis=0, mode='fill', fill_value=0)
        recv = lax.all_to_all(send, 'ep', 0, 0, tiled=True)
        x = recv.reshape(G, el, cap, d).transpose(1, 0, 2, 3).reshape(el, G * cap, d)
        y = _experts(x, ue1, ue3, ue2)
        y = y.reshape(el, G, cap, d).transpose(1, 0, 2, 3).reshape(e, cap, d)
        back = lax.all_to_all(y, 'ep', 0, 0, tiled=True)
        yg = back[ix, sl]
        m = jnp.sum(g[..., None] * yg.astype(f32), axis=1)
        dense = _dense(h0, na, wq, wk, wv, wo, nf, w1, w3, w2)
        return (dense + m).astype(jnp.bfloat16).reshape(b, s, d)

    rows_spec = P(('dp', 'ep'))
    in_specs = (rows_spec,) * 3 + (P(),) * 11 + (P('ep'),) * 3
    return jax.shard_map(local, mesh=mesh, in_specs=in_specs, out_specs=rows_spec, check_vma=False)
```

profile of v0, /device:TPU:112, one launch (start us, length us, event | category | flops | bytes accessed | tf_op | source)
XLA Modules:
  0.0 1892.0 jit_solution(16485000888076227472)
XLA Ops:
  0.0 0.0 copy-start
  0.0 1.4 shift-left_or_fusion
  1.4 1.4 shift-left_or_fusion.1
  2.9 0.8 and_reduce_fusion
  3.7 0.8 multiply_reduce_fusion.1
  4.5 0.2 copy.45
  4.7 0.3 reshape.352
  5.1 0.3 reshape.354
  5.4 23.0 %scatter_custom_fusion = s32[12288]{0:T(1024)S(1)} fusion(s32[6144]{0:T(1024)S(1)} %reshape.352, s32[6144]{0:T(1024)S(1)} %reshape.354, s32[]{:T(128)} %constant.60.clone.1), kind=kCustom, calls=%fused_computation.81 | custom fusion | bytes 49156
  28.5 0.1 reshape.330
  28.6 0.7 convert_element_type.133
  29.3 3.1 fusion.16
  32.4 0.0 copy-start.16
  32.4 0.1 reshape.334
  32.5 5.2 fusion.18
  37.7 94.1 %gather_fusion = bf16[12288,2048]{1,0:T(8,128)(2,1)} fusion(bf16[1024,2048]{1,0:T(8,128)(2,1)} %fusion.18, s32[12288]{0:T(1024)S(1)} %broadcast_clamp_fusion), kind=kCustom, calls=%fused_computation | custom fusion | bytes 100712448 | tf_op jit(solution)/shard_map/jit(_take)/gather | solution.py:81
  131.8 0.0 copy-done.16
  131.8 33.8 %broadcast_select_fusion = bf16[64,192,2048]{2,1,0:T(8,128)(2,1)} fusion(bf16[64,192,2048]{2,1,0:T(8,128)(2,1)} %bitcast.121, pred[64,192]{1,0:T(8,128)(4,1)S(1)} %compare_and_fusion), kind=kLoop, calls=%fused_computation.11 | loop fusion | flops 25165824 | bytes 100675584 | tf_op jit(solution)/shard_map/jit(_take)/select_n | solution.py:81
  165.5 9.1 all-to-all-start
  174.6 1.0 copy.43
  175.7 0.2 copy.44
  175.9 0.3 reshape.346
  176.2 3.6 fusion.64
  179.8 0.0 copy-start.19
  179.8 49.3 %gather_fusion.2 = f32[6144]{0:T(1024)S(1)} fusion(f32[1024,64]{0,1:T(8,128)S(1)} %fusion.64, s32[6144]{0:T(1024)S(1)} %reshape.346), kind=kCustom, calls=%fused_computation.2 | custom fusion | bytes 98304 | tf_op jit(solution)/shard_map/jit(take_along_axis)/gather | solution.py:53
  229.1 0.5 reshape.349
  229.6 12.5 copy.54
  242.1 12.3 copy.53
  254.5 0.2 fusion.60
  254.7 0.0 slice-start
  254.7 1.0 fusion.53
  255.7 1.8 multiply_cosine_fusion
  257.5 0.0 slice-start.2
  257.5 14.8 fusion.38
  272.3 11.3 fusion.35
  283.6 11.1 fusion.32
  294.8 423.9 %all-to-all-done = bf16[64,192,2048]{2,1,0:T(8,128)(2,1)} async-done(((bf16[64,192,2048]{2,1,0:T(8,128)(2,1)}), bf16[64,192,2048]{2,1,0:T(8,128)(2,1)}, u32[]{:S(2)}, u32[]{:S(2)}) %all-to-all-start) | async-done | bytes 50331680 | tf_op jit(solution)/shard_map/all_to_all | solution.py:82
  718.7 33.3 %copy.46 = bf16[8,8,192,2048]{3,2,1,0:T(8,128)(2,1)} copy(bf16[8,8,192,2048]{3,2,0,1:T(8,128)(2,1)} %bitcast.26) | data formatting | bytes 100663296 | tf_op jit(solution)/shard_map/transpose | solution.py:83
  752.0 87.7 %fusion.65 = f32[8,1536,1408]{2,1,0:T(8,128)} fusion(bf16[8,1536,2048]{2,1,0:T(8,128)(2,1)} %bitcast.122, bf16[8,2048,1408]{2,1,0:T(8,128)(2,1)} %param.31), kind=kOutput, calls=%fused_computation.94 | convolution fusion | flops 70866960384 | bytes 165675008 | tf_op jit(solution)/shard_map/ecd,edf->ecf/dot_general | solution.py:59
  839.8 94.8 %fusion.2 = bf16[8,1536,1408]{2,1,0:T(8,128)(2,1)} fusion(bf16[8,1536,2048]{2,1,0:T(8,128)(2,1)} %bitcast.123, bf16[8,2048,1408]{2,1,0:T(8,128)(2,1)} %param.32, f32[8,1536,1408]{2,1,0:T(8,128)} %fusion.65), kind=kOutput, calls=%fused_computation.13 | convolution fusion | flops 70970769408 | bytes 200278016 | tf_op jit(solution)/shard_map/ecd,edf->ecf/dot_general | solution.py:60
  934.6 87.9 %convolution_convert_fusion = bf16[8,1536,2048]{2,1,0:T(8,128)(2,1)} fusion(bf16[8,1536,1408]{2,1,0:T(8,128)(2,1)} %fusion.2, bf16[8,1408,2048]{2,1,0:T(8,128)(2,1)} %param.33), kind=kOutput, calls=%fused_computation.14 | convolution fusion | flops 70892126208 | bytes 131072000 | tf_op jit(solution)/shard_map/ecf,efd->ecd/dot_general | solution.py:62
  1022.5 33.4 %copy.47 = bf16[8,8,192,2048]{3,2,1,0:T(8,128)(2,1)} copy(bf16[8,8,192,2048]{3,2,0,1:T(8,128)(2,1)} %bitcast.124) | data formatting | bytes 100663296 | tf_op jit(solution)/shard_map/transpose | solution.py:85
  1055.9 9.3 all-to-all-start.1
  1065.2 0.0 copy-start.20
  1065.2 0.3 iota_compare_fusion
  1065.5 0.2 copy.48
  1065.8 0.9 reshape.340
  1066.7 6.4 copy.52
  1073.1 0.6 convert_element_type.130
  1073.7 9.1 fusion.46
  1082.8 26.5 %fusion.1 = (f32[16,1024]{1,0:T(8,128)S(1)}, f32[16,1024,1024]{2,1,0:T(8,128)}) fusion(pred[1024,1024]{0,1:T(8,128)(4,1)S(1)} %iota_compare_fusion, bf16[1024,16,64]{0,2,1:T(8,128)(2,1)} %get-tuple-element.8, bf16[1024,16,64]{0,2,1:T(8,128)(2,1)S(1)} %get-tuple-element.7, bf16[1024,16,64]{0,2,1:T(8,128)(2,1)} %get-tuple-element.11, ...), kind=kOutput, calls=%fused_computation.10 | convolution fusion | flops 4362059776 | bytes 76611584 | tf_op jit(solution)/shard_map/bqgrd,bkgd->bgrqk/dot_general | solution.py:37
  1109.4 21.6 %fusion = f32[16,1024]{1,0:T(8,128)S(1)} fusion(f32[16,1024,1024]{2,1,0:T(8,128)} %get-tuple-element.18, f32[16,1024]{1,0:T(8,128)S(1)} %get-tuple-element.17, pred[1024,1024]{0,1:T(8,128)(4,1)S(1)} %iota_compare_fusion), kind=kLoop, calls=%fused_computation.9 | loop fusion | flops 67092480 | bytes 68288512 | tf_op jit(solution)/shard_map/reduce_sum | solution.py:40
  1130.9 28.5 %fusion.41 = bf16[16,128,1024]{2,1,0:T(8,128)(2,1)} fusion(bf16[1024,16,128]{0,2,1:T(8,128)(2,1)} %bitcast.131, f32[16,1024]{1,0:T(8,128)S(1)} %fusion, f32[16,1024]{1,0:T(8,128)S(1)} %get-tuple-element.17, f32[16,1024,1024]{2,1,0:T(8,128)} %get-tuple-element.18, pred[1024,1024]{0,1:T(8,128)(4,1)S(1)} %iota_compare_fusion), kind=kOutput, calls=%fused_computation.58 | convolution fusion | flops 4380950528 | bytes 76677120 | tf_op jit(solution)/shard_map/bgrqk,bkgd->bqgrd/dot_general | solution.py:41
  1159.5 14.3 fusion.9
  1173.7 0.0 copy-start.21
  1173.8 1.5 fusion.52
  1175.3 0.6 copy-done.21
  1175.9 54.6 %fusion.50 = f32[1024,10944]{0,1:T(8,128)} fusion(bf16[2048,10944]{0,1:T(8,128)(2,1)} %param.26, bf16[1024,2048]{1,0:T(8,128)(2,1)S(1)} %get-tuple-element.20, f32[2048]{0:T(1024)S(1)} %copy-done.18, f32[1024]{0:T(1024)S(1)} %add_rsqrt_fusion), kind=kOutput, calls=%fused_computation.64 | convolution fusion | flops 45910851584 | bytes 93859840 | tf_op jit(solution)/shard_map/dot_general | solution.py:44
  1230.5 65.3 %multiply_convert_fusion.clone.4 = bf16[1024,10944]{0,1:T(8,128)(2,1)} fusion(f32[1024,10944]{0,1:T(8,128)} %fusion.50, bf16[2048,10944]{0,1:T(8,128)(2,1)} %param.27, bf16[1024,2048]{1,0:T(8,128)(2,1)} %copy-done.21, f32[2048]{0:T(1024)S(1)} %copy-done.18, f32[1024]{0:T(1024)S(1)} %add_rsqrt_fusion), kind=kOutput, calls=%fused_computation.12.clone.clone.clone.1 | convolution fusion | flops 45978091520 | bytes 116273152 | tf_op jit(solution)/shard_map/dot_general | solution.py:44
  1295.8 313.2 %all-to-all-done.1 = bf16[64,192,2048]{2,1,0:T(8,128)(2,1)} async-done(((bf16[64,192,2048]{2,1,0:T(8,128)(2,1)}), bf16[64,192,2048]{2,1,0:T(8,128)(2,1)}, u32[]{:S(2)}, u32[]{:S(2)}) %all-to-all-start.1) | async-done | bytes 50331680 | tf_op jit(solution)/shard_map/all_to_all | solution.py:86
  1609.0 150.1 %gather_fusion.1 = bf16[6144,2048]{1,0:T(8,128)(2,1)} fusion(bf16[64,192,2048]{2,1,0:T(8,128)(2,1)} %all-to-all-done.1, s32[6144]{0:T(1024)S(1)} %copy-done.2), kind=kCustom, calls=%fused_computation.1 | custom fusion | bytes 50380800 | tf_op jit(solution)/shard_map/gather | solution.py:87
  1759.1 42.9 %reshape.360 = f32[1024,6,2048]{2,1,0:T(8,128)} reshape(bf16[6144,2048]{1,0:T(8,128)(2,1)} %gather_fusion.1) | data formatting | bytes 75497472 | tf_op jit(solution)/shard_map/convert_element_type | solution.py:88
  1802.0 30.5 %multiply_reduce_fusion = f32[1024,2048]{1,0:T(8,128)} fusion(f32[1024,6,2048]{2,1,0:T(8,128)} %reshape.360, f32[1024,6]{1,0:T(8,128)S(1)} %copy-done.8), kind=kLoop, calls=%fused_computation.6 | loop fusion | flops 23068672 | bytes 58744832 | tf_op jit(solution)/shard_map/reduce_sum | solution.py:88
  1832.5 59.0 %fusion.17 = bf16[1,1024,2048]{2,1,0:T(8,128)(2,1)} fusion(f32[1024,2048]{1,0:T(8,128)} %multiply_reduce_fusion, bf16[1024,2048]{1,0:T(8,128)(2,1)} %copy-done.21, bf16[10944,2048]{1,0:T(8,128)(2,1)} %param.28, bf16[1024,10944]{0,1:T(8,128)(2,1)} %multiply_convert_fusion.clone.4), kind=kOutput, calls=%fused_computation.35 | convolution fusion | flops 45910851584 | bytes 84017152 | tf_op jit(solution)/shard_map/dot_general | solution.py:45
  (55 shorter events, 0.2 us)
Async XLA Ops:
  0.0 176.2 %copy-start = (bf16[2048,64]{0,1:T(8,128)(2,1)S(1)}, bf16[2048,64]{0,1:T(8,128)(2,1)}, u32[]{:S(2)}) copy-start(bf16[2048,64]{0,1:T(8,128)(2,1)} %param.30) | copy-start | bytes 786436
  32.4 99.4 %copy-start.16 = (f32[1024]{0:T(1024)}, f32[1024]{0:T(1024)S(1)}, u32[]{:S(2)}) copy-start(f32[1024]{0:T(1024)S(1)} %add_rsqrt_fusion.1) | copy-start | bytes 12292
  165.5 9.1 copy-start.10
  165.5 10.1 copy-start.12
  165.5 553.2 %all-to-all-start = ((bf16[64,192,2048]{2,1,0:T(8,128)(2,1)}), bf16[64,192,2048]{2,1,0:T(8,128)(2,1)}, u32[]{:S(2)}, u32[]{:S(2)}) async-start(bf16[64,192,2048]{2,1,0:T(8,128)(2,1)} %broadcast_select_fusion), calls=%async_computation | async-start | bytes 100663296 | tf_op jit(solution)/shard_map/all_to_all | solution.py:82
  179.8 49.8 %copy-start.19 = (bf16[2048]{0:T(1024)(128)(2,1)S(1)}, bf16[2048]{0:T(1024)(128)(2,1)}, u32[]{:S(2)}) copy-start(bf16[2048]{0:T(1024)(128)(2,1)} %param.20) | copy-start | bytes 12292
  229.6 25.1 %copy-start.6 = (f32[1024,6]{1,0:T(8,128)}, f32[1024,6]{1,0:T(8,128)S(1)}, u32[]{:S(2)}) copy-start(f32[1024,6]{1,0:T(8,128)S(1)} %reshape.349) | copy-start | bytes 73732
  242.1 12.3 copy-start.4
  242.1 15.4 copy-start.17
  254.7 17.6 copy-start.13
  254.7 17.6 slice-start
  257.5 14.8 copy-start.3
  257.5 14.8 slice-start.1
  257.5 26.1 %slice-start.2 = ((s8[8388608]{0:T(1024)(128)(4,1)}), s8[4194304]{0:T(1024)(128)(4,1)S(1)}, s32[]{:S(2)}) async-start(s8[8388608]{0:T(1024)(128)(4,1)} %bitcast.132), calls=%async_computation.4 | async-start | bytes 8388608
  272.3 11.3 slice-start.3
  1055.9 9.6 copy-start.11
  1055.9 553.1 %all-to-all-start.1 = ((bf16[64,192,2048]{2,1,0:T(8,128)(2,1)}), bf16[64,192,2048]{2,1,0:T(8,128)(2,1)}, u32[]{:S(2)}, u32[]{:S(2)}) async-start(bf16[64,192,2048]{2,1,0:T(8,128)(2,1)} %bitcast.120), calls=%async_computation.1 | async-start | bytes 100663296 | tf_op jit(solution)/shard_map/all_to_all | solution.py:86
  1065.2 7.9 copy-start.20
  1065.2 8.5 copy-start.9
  1159.4 14.3 copy-start.5
  1159.4 14.3 copy-start.7
  1159.4 14.3 copy-start.14
  1159.4 14.4 copy-start.15
  1159.4 16.5 copy-start.18
  1173.7 2.2 copy-start.21
  1230.5 378.5 %copy-start.2 = (s32[6144]{0:T(1024)S(1)}, s32[6144]{0:T(1024)}, u32[]{:S(2)}) copy-start(s32[6144]{0:T(1024)} %reshape.340) | copy-start | bytes 73732
  1759.1 42.9 %copy-start.8 = (f32[1024,6]{1,0:T(8,128)S(1)}, f32[1024,6]{1,0:T(8,128)}, u32[]{:S(2)}) copy-start(f32[1024,6]{1,0:T(8,128)} %fusion.52) | copy-start | bytes 73732
  1832.5 59.0 %copy-start.1 = (bf16[2048,64]{0,1:T(8,128)(2,1)S(1)}, bf16[2048,64]{0,1:T(8,128)(2,1)}, u32[]{:S(2)}) copy-start(bf16[2048,64]{0,1:T(8,128)(2,1)} %param.30) | copy-start | bytes 786436
where the time goes:
time: 1900 us; the launch traced here: 1890 us
  waiting for transfers between devices  737 us (39%)
  matrix products  560 us (29%)
  local copies, waits for them, and re-layouts  462 us (24%)
  other arithmetic  114 us (6%)
    all_to_all x1, waiting for transfers between devices, local(): recv = lax.all_to_all(send, 'ep', 0, 0, tiled=True)  424 us
    all_to_all x1, waiting for transfers between devices, local(): back = lax.all_to_all(y, 'ep', 0, 0, tiled=True)  313 us
    gather x1, local copies, waits for them, and re-layouts, local(): yg = back[ix, sl]  150 us
    dot_general x1, matrix products, _experts(): h3 = jnp.einsum('ecd,edf->ecf', x, ue3, preferred_element_type=f32)  94.8 us
    gather x1, local copies, waits for them, and re-layouts, local(): send = jnp.take(u, tok, axis=0, mode='fill', fill_value=0)  94.1 us
    dot_general x1, matrix products, _experts(): jnp.einsum('ecf,efd->ecd', hid, ue2, preferred_element_type=f32)  87.9 us
    dot_general x1, matrix products, _experts(): h1 = jnp.einsum('ecd,edf->ecf', x, ue1, preferred_element_type=f32)  87.7 us
    dot_general x1, matrix products, _dense(): jnp.dot(z, w3, preferred_element_type=f32)  65.3 us
  transfers between devices with their start and end apart: 2, of which 2 were waited for; matrix products, arithmetic and copies ran while one was open for 18% of the time, Pallas kernels for 0%

commit v1 on v0

v1 whole, which is shorter than its diff:
```python
import functools

import jax
import jax.numpy as jnp
from jax import lax
from jax.experimental import pallas as pl
from jax.experimental.pallas import tpu as pltpu
from jax.sharding import PartitionSpec as P

HEAD = 128
EPS = 1e-6
ROPE_BASE = 10000.0
CHUNKS = 2
GR = 16
BG = 256
BM = 384
TB = 128
WIN = 64
F32, BF = jnp.float32, jnp.bfloat16


def _rms(x, w):
    xf = x.astype(F32)
    r = lax.rsqrt(jnp.mean(xf * xf, axis=-1, keepdims=True) + EPS)
    return (xf * r * w.astype(F32)).astype(BF)


def _attn_kernel(scale, qb, q_ref, k_ref, v_ref, cos_ref, sin_ref, o_ref):
    cos, sin = cos_ref[...], sin_ref[...]
    half = HEAD // 2

    def rope(x):
        return (x * cos + pltpu.roll(x, half, 1) * sin).astype(BF)

    q, k, v = rope(q_ref[...]), rope(k_ref[...]), v_ref[...]
    n = q.shape[0] // qb
    for i in range(n):
        kv = (i + 1) * qb
        s = lax.dot_general(q[i * qb:(i + 1) * qb], k[:kv], (((1,), (1,)), ((), ())),
                            preferred_element_type=F32) * scale
        row = lax.broadcasted_iota(jnp.int32, (qb, kv), 0) + i * qb
        col = lax.broadcasted_iota(jnp.int32, (qb, kv), 1)
        s = jnp.where(row >= col, s, -jnp.inf)
        p = jnp.exp(s - jnp.max(s, axis=-1, keepdims=True))
        p = (p / jnp.sum(p, axis=-1, keepdims=True)).astype(BF)
        o = jnp.dot(p, v[:kv], preferred_element_type=F32)
        o_ref[i * qb:(i + 1) * qb, :] = o.astype(BF)


def _attention(q, k, v, cos, sin):
    s, dq = q.shape
    blk = pl.BlockSpec((s, HEAD), lambda h: (0, h))
    tab = pl.BlockSpec((s, HEAD), lambda h: (0, 0))
    return pl.pallas_call(
        functools.partial(_attn_kernel, HEAD ** -0.5, min(256, s)),
        out_shape=jax.ShapeDtypeStruct((s, dq), BF),
        grid=(dq // HEAD,),
        in_specs=[blk, blk, blk, tab, tab],
        out_specs=blk,
        compiler_params=pltpu.CompilerParams(vmem_limit_bytes=40 * 2**20),
        cost_estimate=pl.CostEstimate(flops=4 * s * s * dq, bytes_accessed=12 * s * dq, transcendentals=s * s * dq // HEAD),
        name="attention",
    )(q, k, v, cos, sin)


def _gather_kernel(ng, ge, gr0, gdst, stot, u_ref, rk_ref, x_hbm, xbuf, sem):
    s = pl.program_id(0)
    tc = u_ref.shape[0]
    per = BG // GR
    total = stot[s]
    iota = lax.broadcasted_iota(jnp.int32, (GR, tc), 0)

    def copies(m, act):
        slot = lax.rem(m, 2)
        for k in range(per):
            g = m * per + k

            @pl.when(g < total)
            def _():
                act(pltpu.make_async_copy(
                    xbuf.at[slot, pl.ds(k * GR, GR), :],
                    x_hbm.at[pl.ds(pl.multiple_of(gdst[s, g] * GR, GR), GR), :],
                    sem.at[slot, k]))

    def tile(m, _):
        @pl.when(m >= 2)
        def _():
            copies(m - 2, lambda c: c.wait())

        parts = []
        for k in range(per):
            g = m * per + k
            row = rk_ref[0, pl.ds(ge[s, g], 1), :]
            pos = iota + gr0[s, g]
            parts.append((pos.astype(F32) == row).astype(F32).astype(BF))
        onehot = jnp.concatenate(parts, axis=0)
        xbuf[lax.rem(m, 2)] = jnp.dot(onehot, u_ref[...], preferred_element_type=F32).astype(BF)
        copies(m, lambda c: c.start())
        return 0

    tiles = lax.div(total + per - 1, per)
    lax.fori_loop(0, tiles, tile, 0)

    @pl.when(tiles >= 2)
    def _():
        copies(tiles - 2, lambda c: c.wait())

    @pl.when(tiles >= 1)
    def _():
        copies(tiles - 1, lambda c: c.wait())


def _gather(u, rk, tabs, rows, ng):
    srcs, el, tc = rk.shape
    d = u.shape[1]
    return pl.pallas_call(
        functools.partial(_gather_kernel, ng),
        out_shape=jax.ShapeDtypeStruct((rows, d), BF),
        grid_spec=pltpu.PrefetchScalarGridSpec(
            num_scalar_prefetch=4,
            grid=(srcs,),
            in_specs=[pl.BlockSpec((tc, d), lambda s, *_: (s, 0)),
                      pl.BlockSpec((1, el, tc), lambda s, *_: (s, 0, 0))],
            out_specs=pl.BlockSpec(memory_space=pl.ANY),
            scratch_shapes=[pltpu.VMEM((2, BG, d), BF), pltpu.SemaphoreType.DMA((2, BG // GR))],
        ),
        compiler_params=pltpu.CompilerParams(vmem_limit_bytes=48 * 2**20),
        cost_estimate=pl.CostEstimate(flops=2 * rows * tc * d, bytes_accessed=4 * rows * d, transcendentals=0),
        name="gather_rows",
    )(*tabs, u, rk)


def _expert_kernel(te, tv, nt, x_ref, w1_ref, w3_ref, w2_ref, y_ref):
    i = pl.program_id(0)

    @pl.when(i < nt[0])
    def _():
        x = x_ref[...]
        h1 = jnp.dot(x, w1_ref[0], preferred_element_type=F32)
        h3 = jnp.dot(x, w3_ref[0], preferred_element_type=F32)
        hid = (jax.nn.silu(h1) * h3).astype(BF)
        y = jnp.dot(hid, w2_ref[0], preferred_element_type=F32)
        row = lax.broadcasted_iota(jnp.int32, (y.shape[0], 1), 0)
        y_ref[...] = jnp.where(row < tv[i], y, 0.0).astype(BF)


def _experts(x, ue1, ue3, ue2, te, tv, nt, max_tiles):
    el, d, fe = ue1.shape

    def rowmap(i, te, tv, nt):
        return (jnp.minimum(i, nt[0] - 1), 0)

    def wmap(i, te, tv, nt):
        return (te[i], 0, 0)

    rows = max_tiles * BM
    return pl.pallas_call(
        _expert_kernel,
        out_shape=jax.ShapeDtypeStruct((rows, d), BF),
        grid_spec=pltpu.PrefetchScalarGridSpec(
            num_scalar_prefetch=3,
            grid=(max_tiles,),
            in_specs=[pl.BlockSpec((BM, d), rowmap),
                      pl.BlockSpec((1, d, fe), wmap),
                      pl.BlockSpec((1, d, fe), wmap),
                      pl.BlockSpec((1, fe, d), wmap)],
            out_specs=pl.BlockSpec((BM, d), rowmap),
        ),
        compiler_params=pltpu.CompilerParams(vmem_limit_bytes=61 * 2**20),
        cost_estimate=pl.CostEstimate(flops=3 * rows * d * fe, bytes_accessed=6 * el * d * fe, transcendentals=rows * fe),
        name="experts",
    )(te, tv, nt, x, ue1, ue3, ue2)


def _combine_kernel(nb, st, tend, nwin, y_hbm, pos_ref, g_ref, o_ref, ybuf, sem):
    s, b = pl.program_id(0), pl.program_id(1)
    el = pos_ref.shape[1]
    i = s * nb + b
    last = pl.num_programs(0) * nb - 1
    slot = lax.rem(i, 2)

    def start_of(step, e, w):
        return jnp.minimum(st[step, e] + w * WIN, tend[e] - WIN)

    def windows(step, w, sl, act):
        for e in range(el):
            act(pltpu.make_async_copy(
                y_hbm.at[pl.ds(pl.multiple_of(start_of(step, e, w), GR), WIN), :],
                ybuf.at[sl, pl.ds(e * WIN, WIN), :],
                sem.at[sl, e]))

    @pl.when(i == 0)
    def _():
        windows(0, 0, 0, lambda c: c.start())

    @pl.when(i < last)
    def _():
        windows(i + 1, 0, 1 - slot, lambda c: c.start())

    gates = g_ref[0]
    g1 = gates.astype(BF).astype(F32)
    r1 = gates - g1
    g2 = r1.astype(BF).astype(F32)
    terms = (g1, g2, r1 - g2)
    iota = lax.broadcasted_iota(jnp.int32, (WIN, TB), 0)

    def part(w, sl):
        cols = []
        for term in terms:
            rows = []
            for e in range(el):
                pos = pos_ref[0, e:e + 1, :]
                lo = st[i, e] + w * WIN
                ok = (pos >= lo) & (pos < lo + WIN)
                rel = jnp.where(ok, pos - start_of(i, e, w), -1)
                rows.append(jnp.where(iota == rel, term[e:e + 1, :], 0.0).astype(BF))
            cols.append(jnp.concatenate(rows, axis=0))
        wt = jnp.concatenate(cols, axis=1)
        r = lax.dot_general(wt, ybuf[sl], (((0,), (0,)), ((), ())), preferred_element_type=F32)
        return r[:TB] + r[TB:2 * TB] + r[2 * TB:]

    windows(i, 0, slot, lambda c: c.wait())
    o_ref[...] = part(0, slot)

    def more(w, _):
        windows(i, w, 2, lambda c: c.start())
        windows(i, w, 2, lambda c: c.wait())
        o_ref[...] += part(w, 2)
        return 0

    lax.fori_loop(1, nwin[i], more, 0)


def _combine(y, pos, gate, st, tend, nwin):
    srcs, el, tc = pos.shape
    d = y.shape[1]
    nb = tc // TB
    blk = pl.BlockSpec((1, el, TB), lambda s, b, *_: (s, 0, b))
    return pl.pallas_call(
        functools.partial(_combine_kernel, nb),
        out_shape=jax.ShapeDtypeStruct((srcs * tc, d), F32),
        grid_spec=pltpu.PrefetchScalarGridSpec(
            num_scalar_prefetch=3,
            grid=(srcs, nb),
            in_specs=[pl.BlockSpec(memory_space=pl.ANY), blk, blk],
            out_specs=pl.BlockSpec((TB, d), lambda s, b, *_: (s * nb + b, 0)),
            scratch_shapes=[pltpu.VMEM((3, el * WIN, d), BF), pltpu.SemaphoreType.DMA((3, el))],
        ),
        compiler_params=pltpu.CompilerParams(vmem_limit_bytes=48 * 2**20),
        cost_estimate=pl.CostEstimate(flops=6 * srcs * tc * el * WIN * d, bytes_accessed=4 * srcs * tc * d, transcendentals=0),
        name="combine",
    )(st, tend, nwin, y, pos, gate)


def _excl(x, axis):
    return jnp.cumsum(x, axis=axis) - x


def _tables(rk, cap):
    srcs, el, tc = rk.shape
    i32 = jnp.int32
    nb = tc // TB
    has = (rk >= 0).reshape(srcs, el, nb, TB).sum(-1, dtype=i32)
    hi = jnp.cumsum(has, axis=2)
    lo = hi - has
    gran = (hi[:, :, -1] + GR - 1) // GR
    tot = gran.sum(0)
    tiles = jnp.maximum(1, (tot * GR + BM - 1) // BM)
    tbase = _excl(tiles, 0)
    seg = tbase * (BM // GR) + _excl(gran, 0)
    soff = _excl(gran, 1)
    stot = gran.sum(1)
    ng = el * (cap // GR + (cap % GR > 0)) + BG // GR
    gi = jnp.arange(ng, dtype=i32)
    own = (gi[None, :, None] >= soff[:, None, :]) & (gi[None, :, None] < (soff + gran)[:, None, :])
    eid = jnp.arange(el, dtype=i32)
    ge = jnp.sum(jnp.where(own, eid, 0), -1)
    live = gi[None, :] < stot[:, None]
    gr0 = jnp.where(live, gi[None, :] - jnp.sum(jnp.where(own, soff[:, None, :], 0), -1), 1 << 16) * GR
    gdst = jnp.sum(jnp.where(own, (seg - soff)[:, None, :], 0), -1) + gi[None, :]
    max_tiles = el * (-(-(srcs * (-(-cap // GR)) * GR) // BM))
    nt = tiles.sum()
    ti = jnp.arange(max_tiles, dtype=i32)
    te = jnp.sum((ti[:, None] >= (tbase + tiles)[None, :]).astype(i32), -1)
    te = jnp.minimum(te, el - 1)
    mine = te[:, None] == eid[None, :]
    tv = jnp.sum(jnp.where(mine, (tot * GR + tbase * BM)[None, :], 0), -1) - ti * BM
    tend = (tbase + tiles) * BM
    lo16 = lo // GR * GR
    st = (lo16 + seg[:, :, None] * GR).transpose(0, 2, 1).reshape(srcs * nb, el)
    nwin = jnp.max((hi - lo16 + WIN - 1) // WIN, axis=1).reshape(srcs * nb)
    pos = jnp.where(rk >= 0, rk.astype(i32) + seg[:, :, None] * GR, -1)
    return (ge, gr0, gdst, stot), (te, tv, nt.reshape(1)), (st, tend, nwin), pos, max_tiles, ng


def solution(mesh):
    G = mesh.shape['ep']

    def local(h0, idx, slot, na, wq, wk, wv, wo, nf, w1, w3, w2, nm, wr, ue1, ue3, ue2):
        b, s, d = h0.shape
        t = b * s
        k = idx.shape[-1]
        el = ue1.shape[0]
        e = el * G
        cap = 2 * t * k // e
        tc = t // CHUNKS
        h = h0.reshape(t, d)

        u = _rms(h, nm)
        us = [lax.all_gather(u[c * tc:(c + 1) * tc], 'ep', axis=0, tiled=True) for c in range(CHUNKS)]

        idxt = idx.reshape(t, k).T
        hit = (idxt[:, None, :] == jnp.arange(e, dtype=jnp.int32)[None, :, None]).any(0)
        logits = lax.dot_general(wr, u, (((0,), (1,)), ((), ())), preferred_element_type=F32)
        top = jnp.max(jnp.where(hit, logits, -jnp.inf), axis=0, keepdims=True)
        ex = jnp.where(hit, jnp.exp(logits - top), 0.0)
        gate = ex / jnp.sum(ex, axis=0, keepdims=True)
        before = (jnp.arange(tc)[:, None] < jnp.arange(tc)[None, :]).astype(BF)
        rank = jnp.dot(hit.astype(BF).reshape(e * CHUNKS, tc), before, preferred_element_type=F32).reshape(e, t)
        rank = jnp.where(hit, rank, -1.0)
        route = jnp.concatenate([rank.reshape(G, el, t), gate.reshape(G, el, t)], axis=1)
        route = lax.all_to_all(route, 'ep', 0, 0, tiled=True)

        pos = jnp.arange(s).astype(F32)
        inv = ROPE_BASE ** (-2.0 * jnp.arange(HEAD // 2).astype(F32) / HEAD)
        ang = pos[:, None] * inv[None, :]
        cos, sin = jnp.cos(ang), jnp.sin(ang)
        cosf = jnp.concatenate([cos, cos], axis=1)
        sinf = jnp.concatenate([-sin, sin], axis=1)
        x = _rms(h, na)
        q = jnp.dot(x, wq, preferred_element_type=F32)
        kk = jnp.dot(x, wk, preferred_element_type=F32)
        v = jnp.dot(x, wv, preferred_element_type=F32).astype(BF)
        o = jnp.concatenate([_attention(q[i * s:(i + 1) * s], kk[i * s:(i + 1) * s], v[i * s:(i + 1) * s], cosf, sinf)
                             for i in range(b)], axis=0)
        a = (h.astype(F32) + jnp.dot(o, wo, preferred_element_type=F32)).astype(BF)

        ms = []
        gatekeeper = a
        for c in range(CHUNKS):
            rk = route[:, :el, c * tc:(c + 1) * tc]
            gt = route[:, el:, c * tc:(c + 1) * tc]
            gtab, etab, ctab, ps, max_tiles, ng = _tables(rk, cap)
            uc, gatekeeper = lax.optimization_barrier((us[c], gatekeeper))
            xr = _gather(uc, rk, gtab, max_tiles * BM, ng)
            y = _experts(xr, ue1, ue3, ue2, *etab, max_tiles)
            part = _combine(y, ps, gt, *ctab)
            part, gatekeeper = lax.optimization_barrier((part, gatekeeper))
            ms.append(lax.psum_scatter(part, 'ep', scatter_dimension=0, tiled=True))
        m = jnp.concatenate(ms, axis=0)

        a = gatekeeper
        z = _rms(a, nf)
        hid = (jax.nn.silu(jnp.dot(z, w1, preferred_element_type=F32)) * jnp.dot(z, w3, preferred_element_type=F32)).astype(BF)
        af = a.astype(F32) + jnp.dot(hid, w2, preferred_element_type=F32)
        af, m = lax.optimization_barrier((af, m))
        return (af + m).astype(BF).reshape(b, s, d)

    rows_spec = P(('dp', 'ep'))
    in_specs = (rows_spec,) * 3 + (P(),) * 11 + (P('ep'),) * 3
    return jax.shard_map(local, mesh=mesh, in_specs=in_specs, out_specs=rows_spec, check_vma=False)
```

time: 1900 us -> 770 us (0.41)
  waiting for transfers between devices: 737 us -> 0.92 us
  Pallas kernels: 0 us -> 462 us
  local copies, waits for them, and re-layouts: 462 us -> 6.23 us
  matrix products: 560 us -> 233 us
  other arithmetic: 114 us -> 39.2 us
    all_to_all x2 -> x1, waiting for transfers between devices: 737 us -> 0.01 us  [local(): route = lax.all_to_all(route, 'ep', 0, 0, tiled=True)]
    pallas_call x0 -> x7, Pallas kernels: none -> 462 us  [the longest x2 262 us: _experts(): pl.pallas_call(_expert_kernel, out_shape=jax.ShapeDtypeStruct((rows, d),...]
    dot_general x13 -> x9, matrix products: 560 us -> 233 us  [the longest x1 65.2 us: local(): jnp.dot(z, w3, preferred_element_type=F32)]
    gather x6 -> x0, local copies, waits for them, and re-layouts: 295 us -> none  [the longest x1 150 us: local(): yg = back[ix, sl]]
    transpose x2 -> x0, local copies, waits for them, and re-layouts: 66.7 us -> none  [the longest x1 33.4 us: local(): y = y.reshape(el, G, cap, d).transpose(1, 0, 2, 3).reshape(e, cap, d)]
    reduce_sum x3 -> x12, other arithmetic: 53 us -> 3.89 us  [the longest x2 1.33 us: _tables(): nt = tiles.sum()]
    convert_element_type x1 -> x0, local copies, waits for them, and re-layouts: 42.9 us -> none  [local(): m = jnp.sum(g[..., None] * yg.astype(f32), axis=1)]
    select_n x2, other arithmetic: 33.8 us -> 0.12 us  [the longest x1 0.09 us: _tables(): pos = jnp.where(rk >= 0, rk.astype(i32) + seg[:, :, None] * GR, -1)]
  transfers between devices with their start and end apart: 2 -> 5, of which waited for: 2 -> 0; matrix products, arithmetic and copies ran while one was open for 18% -> 33% of each run, Pallas kernels for 0% -> 61%
where the time goes in v1:
time: 770 us; the launch traced here: 762 us
  Pallas kernels  462 us (60%)
  matrix products  233 us (30%)
  other arithmetic  39.2 us (5%)
  between operations  14.1 us (2%)
    pallas_call x2, Pallas kernels, _experts(): pl.pallas_call(_expert_kernel, out_shape=jax.ShapeDtypeStruct((rows, d),...  262 us
    pallas_call x2, Pallas kernels, _combine(): pl.pallas_call(functools.partial(_combine_kernel, nb), out_shape=jax.Shap...  102 us
    dot_general x1, matrix products, local(): jnp.dot(z, w3, preferred_element_type=F32)  65.2 us
    dot_general x1, matrix products, local(): af = a.astype(F32) + jnp.dot(hid, w2, preferred_element_type=F32)  59.8 us
    pallas_call x2, Pallas kernels, _gather(): pl.pallas_call(functools.partial(_gather_kernel, ng), out_shape=jax.Shape...  57.4 us
    dot_general x1, matrix products, local(): jnp.dot(z, w1, preferred_element_type=F32)  56 us
    pallas_call x1, Pallas kernels, _attention(): pl.pallas_call(functools.partial(_attn_kernel, HEAD ** (-0.5), min(256, s...  40.6 us
  transfers between devices with their start and end apart: 5, of which 0 were waited for; matrix products, arithmetic and copies ran while one was open for 33% of the time, Pallas kernels for 61%

profile of v1, /device:TPU:112, one launch (start us, length us, event | category | flops | bytes accessed | tf_op | source)
XLA Modules:
  0.0 761.5 jit_solution(10841549965071396640)
XLA Ops:
  6.6 3.1 fusion.7
  9.7 0.7 convert_element_type.96
  10.4 3.2 fusion.2
  13.6 2.0 copy-done.3
  15.6 2.5 fusion.84
  18.2 0.7 all-gather.3.cloned.1.call-update
  19.0 0.2 fusion.10
  19.3 0.2 fusion.15
  19.5 0.1 reshape.379
  19.6 3.6 select_reduce_fusion
  23.3 0.1 fusion.16
  23.3 0.1 divide_bitcast_fusion
  23.4 0.8 pad_maximum_fusion.1
  24.3 5.3 all-to-all-start
  29.7 1.9 fusion.17
  31.6 0.3 pad_maximum_fusion.2
  32.0 13.1 %convolution_convert_fusion.v_ref = bf16[1024,2048]{1,0:T(8,128)(2,1)S(1)} fusion(bf16[2048,2048]{1,0:T(8,128)(2,1)} %param.22, bf16[1,1024,2048]{2,1,0:T(8,128)(2,1)} %param.17, f32[2048]{0:T(1024)S(1)} %convert_element_type.104, f32[1024]{0:T(1024)S(1)} %add_rsqrt_fusion.1), kind=kOutput, calls=%fused_computation.19 | convolution fusion | flops 8600420352 | bytes 16789504 | tf_op jit(solution)/shard_map/dot_general | solution.py:333
  45.1 11.2 %fusion.78.k_ref = f32[1024,2048]{1,0:T(8,128)} fusion(bf16[2048,2048]{1,0:T(8,128)(2,1)S(1)} %bitcast.147, bf16[1,1024,2048]{2,1,0:T(8,128)(2,1)S(1)} %copy-done.4, f32[2048]{0:T(1024)S(1)} %convert_element_type.104, f32[1024]{0:T(1024)S(1)} %add_rsqrt_fusion.1), kind=kOutput, calls=%fused_computation.210 | convolution fusion | flops 8598323200 | bytes 20983808 | tf_op jit(solution)/shard_map/dot_general | solution.py:332
  56.3 13.4 %fusion.80.q_ref = f32[1024,2048]{1,0:T(8,128)} fusion(bf16[2048,2048]{1,0:T(8,128)(2,1)} %param.20, bf16[1,1024,2048]{2,1,0:T(8,128)(2,1)S(1)} %copy-done.4, f32[2048]{0:T(1024)S(1)} %convert_element_type.104, f32[1024]{0:T(1024)S(1)} %add_rsqrt_fusion.1), kind=kOutput, calls=%fused_computation.211 | convolution fusion | flops 8598323200 | bytes 20983808 | tf_op jit(solution)/shard_map/dot_general | solution.py:331
  69.7 40.6 %attention.1 = bf16[1024,2048]{1,0:T(8,128)(2,1)S(1)} custom-call(f32[1024,2048]{1,0:T(8,128)} %fusion.80.q_ref, f32[1024,2048]{1,0:T(8,128)} %fusion.78.k_ref, bf16[1024,2048]{1,0:T(8,128)(2,1)S(1)} %convolution_convert_fusion.v_ref, f32[1024,128]{1,0:T(8,128)S(1)} %get-tuple-element.78.cos_ref, f32[1024,128]{1,0:T(8,128)S(1)} %get-tuple-element.79.sin_ref), custom_call_target="tpu_custom_call" | custom-call | flops 8589934592 | bytes 25165824 | tf_op jit(solution)/shard_map/attention/pallas_call | solution.py:54
  110.3 10.7 %fusion.8 = bf16[1024,2048]{1,0:T(8,128)(2,1)} fusion(bf16[1,1024,2048]{2,1,0:T(8,128)(2,1)S(1)} %copy-done.4, bf16[1024,2048]{1,0:T(8,128)(2,1)S(1)} %attention.1, bf16[2048,2048]{1,0:T(8,128)(2,1)S(1)} %bitcast.149), kind=kOutput, calls=%fused_computation.15 | convolution fusion | flops 8596226048 | bytes 20971520 | tf_op jit(solution)/shard_map/dot_general | solution.py:336
  121.1 1.2 bitcast_reduce_fusion
  122.2 0.3 fusion.37
  122.6 0.1 fusion.82
  122.7 0.2 reduce_window_sum.71
  122.9 0.1 copy.40
  123.0 0.1 reshape.387.nwin
  123.1 0.7 fusion.75
  123.7 0.2 reduce-window.15
  123.9 0.9 fusion.28
  124.8 0.6 fusion.83
  125.4 0.7 fusion.76
  126.1 0.2 reduce-window.14
  126.4 0.5 multiply_add_fusion.1
  126.9 0.6 fusion.22
  127.6 0.1 convert_reduce_fusion
  127.7 0.1 select_reduce_fusion.7
  127.8 0.1 select_reduce_fusion.1
  127.9 0.6 fusion.72.tv
  128.5 0.1 iota_add_fusion
  128.5 0.1 add_select_fusion
  128.7 28.5 %gather_rows.2.x_ref = bf16[12288,2048]{1,0:T(8,128)(2,1)} custom-call(s32[8,112]{1,0:T(8,128)S(1)} %get-tuple-element.29.ge, s32[8,112]{1,0:T(8,128)S(1)} %get-tuple-element.77.gr0, s32[8,112]{1,0:T(8,128)S(1)} %get-tuple-element.76.gdst, s32[8]{0:T(128)S(1)} %get-tuple-element.33.stot, bf16[4096,2048]{1,0:T(8,128)(2,1)} %all-gather.5.cloned.1.call-done.u_ref, ...), custom_call_target="tpu_custom_call" | custom-call | flops 25769803776 | bytes 100663296 | tf_op jit(solution)/shard_map/gather_rows/pallas_call | solution.py:116
  157.2 131.0 %experts.2.y_hbm = bf16[12288,2048]{1,0:T(8,128)(2,1)} custom-call(s32[32]{0:T(128)} %copy-done.19, s32[32]{0:T(128)} %fusion.72.tv, s32[1]{0:T(128)} %bitcast.25.nt, bf16[12288,2048]{1,0:T(8,128)(2,1)} %gather_rows.2.x_ref, bf16[8,2048,1408]{2,1,0:T(8,128)(2,1)} %w1_ref.3, bf16[8,2048,1408]{2,1,0:T(8,128)(2,1)} %w3_ref.3, bf16[8,1408,2048]{2,1,0:T(8,128)(2,1)} %w2_ref.3), custom_call_target="tpu_custom_call" | custom-call | flops 106300440576 | bytes 138412032 | tf_op jit(solution)/shard_map/experts/pallas_call | solution.py:157
  288.2 51.1 %combine.2 = f32[4096,2048]{1,0:T(8,128)} custom-call(s32[32,8]{1,0:T(8,128)S(1)} %bitcast.141, s32[8]{0:T(128)S(1)} %get-tuple-element.64.tend, s32[32]{0:T(128)S(1)} %reshape.387.nwin, bf16[12288,2048]{1,0:T(8,128)(2,1)} %experts.2.y_hbm, s32[8,8,512]{2,1,0:T(8,128)S(1)} %get-tuple-element.56.pos_ref, f32[8,8,512]{2,1,0:T(8,128)S(1)} %get-tuple-element.52.g_ref), custom_call_target="tpu_custom_call" | custom-call | flops 25769803776 | bytes 33554432 | tf_op jit(solution)/shard_map/combine/pallas_call | solution.py:239
  339.5 0.1 reduce-scatter.5.cloned.1.call-start
  339.5 0.5 copy-done.6
  340.0 0.2 reduce_window_sum.67
  340.2 0.1 copy.36
  340.3 0.1 reshape.383.nwin
  340.4 0.1 convert_reduce_fusion.1
  340.5 0.1 select_reduce_fusion.8
  340.6 0.1 select_reduce_fusion.4
  340.7 0.5 fusion.73.tv
  341.2 0.1 iota_add_fusion.1
  341.2 28.9 %gather_rows.3.x_ref = bf16[12288,2048]{1,0:T(8,128)(2,1)} custom-call(s32[8,112]{1,0:T(8,128)S(1)} %get-tuple-element.32.ge, s32[8,112]{1,0:T(8,128)S(1)} %get-tuple-element.75.gr0, s32[8,112]{1,0:T(8,128)S(1)} %get-tuple-element.74.gdst, s32[8]{0:T(128)S(1)} %copy-done.2, bf16[4096,2048]{1,0:T(8,128)(2,1)} %all-gather.3.cloned.1.call-done.u_ref, ...), custom_call_target="tpu_custom_call" | custom-call | flops 25769803776 | bytes 100663296 | tf_op jit(solution)/shard_map/gather_rows/pallas_call | solution.py:116
  370.2 131.0 %experts.3.y_hbm = bf16[12288,2048]{1,0:T(8,128)(2,1)} custom-call(s32[32]{0:T(128)} %copy-done.20, s32[32]{0:T(128)} %fusion.73.tv, s32[1]{0:T(128)} %bitcast.15.nt, bf16[12288,2048]{1,0:T(8,128)(2,1)} %gather_rows.3.x_ref, bf16[8,2048,1408]{2,1,0:T(8,128)(2,1)} %w1_ref.3, bf16[8,2048,1408]{2,1,0:T(8,128)(2,1)} %w3_ref.3, bf16[8,1408,2048]{2,1,0:T(8,128)(2,1)} %w2_ref.3), custom_call_target="tpu_custom_call" | custom-call | flops 106300440576 | bytes 138412032 | tf_op jit(solution)/shard_map/experts/pallas_call | solution.py:157
  501.1 51.2 %combine.3 = f32[4096,2048]{1,0:T(8,128)} custom-call(s32[32,8]{1,0:T(8,128)S(1)} %bitcast.142, s32[8]{0:T(128)S(1)} %get-tuple-element.65.tend, s32[32]{0:T(128)S(1)} %reshape.383.nwin, bf16[12288,2048]{1,0:T(8,128)(2,1)} %experts.3.y_hbm, s32[8,8,512]{2,1,0:T(8,128)S(1)} %get-tuple-element.55.pos_ref, f32[8,8,512]{2,1,0:T(8,128)S(1)} %get-tuple-element.51.g_ref), custom_call_target="tpu_custom_call" | custom-call | flops 25769803776 | bytes 33554432 | tf_op jit(solution)/shard_map/combine/pallas_call | solution.py:239
  552.4 0.6 copy-done.15
  553.0 3.1 fusion.4
  556.1 56.0 %fusion.13 = f32[1024,10944]{0,1:T(8,128)} fusion(bf16[2048,10944]{0,1:T(8,128)(2,1)} %param.25, bf16[1024,2048]{1,0:T(8,128)(2,1)} %fusion.8, f32[2048]{0:T(1024)S(1)} %convert_element_type.113, f32[1024]{0:T(1024)S(1)} %add_rsqrt_fusion), kind=kOutput, calls=%fused_computation.22 | convolution fusion | flops 45910851584 | bytes 93859840 | tf_op jit(solution)/shard_map/dot_general | solution.py:354
  612.1 65.2 %multiply_convert_fusion.clone.4 = bf16[1024,10944]{0,1:T(8,128)(2,1)} fusion(f32[1024,10944]{0,1:T(8,128)} %fusion.13, bf16[2048,10944]{0,1:T(8,128)(2,1)} %param.26, bf16[1024,2048]{1,0:T(8,128)(2,1)} %fusion.8, f32[2048]{0:T(1024)S(1)} %convert_element_type.113, f32[1024]{0:T(1024)S(1)} %add_rsqrt_fusion), kind=kOutput, calls=%fused_computation.clone.clone.clone.1 | convolution fusion | flops 45978091520 | bytes 116273152 | tf_op jit(solution)/shard_map/dot_general | solution.py:354
  677.3 59.8 %convert_add_fusion.1 = f32[1024,2048]{1,0:T(8,128)} fusion(bf16[1024,2048]{1,0:T(8,128)(2,1)} %fusion.8, bf16[10944,2048]{1,0:T(8,128)(2,1)} %param.27, bf16[1024,10944]{0,1:T(8,128)(2,1)} %multiply_convert_fusion.clone.4), kind=kOutput, calls=%fused_computation.4 | convolution fusion | flops 45906657280 | bytes 79822848 | tf_op jit(solution)/shard_map/dot_general | solution.py:355
  737.2 7.9 %pad_maximum_fusion = f32[1024,2048]{1,0:T(8,128)} fusion(f32[512,2048]{1,0:T(8,128)} %reduce-scatter.5.cloned.1.call-done, f32[512,2048]{1,0:T(8,128)} %reduce-scatter.3.cloned.1.call-done), kind=kLoop, calls=%fused_computation.16 | loop fusion | flops 2097152 | bytes 16777216 | tf_op jit(solution)/shard_map/concatenate | solution.py:350
  745.1 9.4 %fusion.9 = bf16[1,1024,2048]{2,1,0:T(8,128)(2,1)} fusion(f32[1024,2048]{1,0:T(8,128)} %convert_add_fusion.1, f32[1024,2048]{1,0:T(8,128)} %pad_maximum_fusion), kind=kLoop, calls=%fused_computation.18 | loop fusion | flops 4194304 | bytes 20971520 | tf_op jit(solution)/shard_map/reshape | solution.py:357
  (83 shorter events, 0.7 us)
Async XLA Ops:
  6.5 13.1 %copy-start = (bf16[2048,64]{0,1:T(8,128)(2,1)S(1)}, bf16[2048,64]{0,1:T(8,128)(2,1)}, u32[]{:S(2)}) copy-start(bf16[2048,64]{0,1:T(8,128)(2,1)} %param.29) | copy-start | bytes 786436
  6.6 122.1 %all-gather.5.cloned.1.call-start = ((), (), s32[]{:S(2)}) async-start(), calls=%async_computation.4 | async-start | bytes 18874368 | tf_op jit(solution)/shard_map/all_gather | solution.py:310
  13.6 2.0 copy-start.3
  15.6 3.4 copy-start.10
  18.1 11.5 %copy-start.14 = (bf16[2048]{0:T(1024)(128)(2,1)S(1)}, bf16[2048]{0:T(1024)(128)(2,1)}, u32[]{:S(2)}) copy-start(bf16[2048]{0:T(1024)(128)(2,1)} %param.19) | copy-start | bytes 12292
  18.2 323.1 %all-gather.3.cloned.1.call-start = ((), (), s32[]{:S(2)}) async-start(), calls=%async_computation.3 | async-start | bytes 18874368 | tf_op jit(solution)/shard_map/all_gather | solution.py:310
  24.3 96.8 %all-to-all-start = ((f32[8,16,1024]{2,1,0:T(8,128)}), f32[8,16,1024]{2,1,0:T(8,128)S(1)}, u32[]{:S(2)}, u32[]{:S(2)}) async-start(f32[8,16,1024]{2,1,0:T(8,128)} %pad_maximum_fusion.1), calls=%async_computation | async-start | bytes 1048576 | tf_op jit(solution)/shard_map/all_to_all | solution.py:322
  29.6 707.6 %reduce-scatter.3.cloned.1.call-start = ((), (), s32[]{:S(2)}) async-start(), calls=%async_computation.5 | async-start | bytes 37748736 | tf_op jit(solution)/shard_map/reduce_scatter | solution.py:349
  31.6 13.5 %slice-start = ((s8[8388608]{0:T(1024)(128)(4,1)}), s8[4194304]{0:T(1024)(128)(4,1)S(1)}, s32[]{:S(2)}) async-start(s8[8388608]{0:T(1024)(128)(4,1)} %bitcast.146), calls=%async_computation.7 | async-start | bytes 8388608
  31.9 13.1 %copy-start.4 = (bf16[1,1024,2048]{2,1,0:T(8,128)(2,1)S(1)}, bf16[1,1024,2048]{2,1,0:T(8,128)(2,1)}, u32[]{:S(2)}) copy-start(bf16[1,1024,2048]{2,1,0:T(8,128)(2,1)} %param.17) | copy-start | bytes 12582916
  32.0 13.1 %slice-start.1 = ((s8[8388608]{0:T(1024)(128)(4,1)}), s8[4194304]{0:T(1024)(128)(4,1)S(1)}, s32[]{:S(2)}) async-start(s8[8388608]{0:T(1024)(128)(4,1)} %bitcast.146), calls=%async_computation.8 | async-start | bytes 8388608
  45.1 65.2 %slice-start.2 = ((s8[8388608]{0:T(1024)(128)(4,1)}), s8[4194304]{0:T(1024)(128)(4,1)S(1)}, s32[]{:S(2)}) async-start(s8[8388608]{0:T(1024)(128)(4,1)} %bitcast.148), calls=%async_computation.9 | async-start | bytes 8388608
  56.3 54.0 %slice-start.3 = ((s8[8388608]{0:T(1024)(128)(4,1)}), s8[4194304]{0:T(1024)(128)(4,1)S(1)}, s32[]{:S(2)}) async-start(s8[8388608]{0:T(1024)(128)(4,1)} %bitcast.148), calls=%async_computation.10 | async-start | bytes 8388608
  125.4 0.9 copy-start.5
  126.3 0.6 copy-start.16
  126.3 0.6 copy-start.8
  126.9 0.8 copy-start.12
  127.7 29.6 %copy-start.19 = (s32[32]{0:T(128)}, s32[32]{0:T(128)S(1)}, u32[]{:S(2)}) copy-start(s32[32]{0:T(128)S(1)} %broadcast_minimum_fusion.te) | copy-start | bytes 388
  339.3 0.7 copy-start.6
  339.3 0.8 copy-start.11
  339.3 1.0 copy-start.7
  339.4 1.0 copy-start.17
  339.4 1.1 copy-start.18
  339.4 1.2 copy-start.9
  339.4 1.2 copy-start.13
  339.4 1.8 copy-start.2
  339.5 397.7 %reduce-scatter.5.cloned.1.call-start = ((), (), s32[]{:S(2)}) async-start(), calls=%async_computation.6 | async-start | bytes 37748736 | tf_op jit(solution)/shard_map/reduce_scatter | solution.py:349
  340.4 29.7 %copy-start.20 = (s32[32]{0:T(128)}, s32[32]{0:T(128)S(1)}, u32[]{:S(2)}) copy-start(s32[32]{0:T(128)S(1)} %broadcast_minimum_fusion.1.te) | copy-start | bytes 388
  552.3 0.7 copy-start.15
  737.1 17.3 %copy-start.1 = (bf16[2048,64]{0,1:T(8,128)(2,1)S(1)}, bf16[2048,64]{0,1:T(8,128)(2,1)}, u32[]{:S(2)}) copy-start(bf16[2048,64]{0,1:T(8,128)(2,1)} %param.29) | copy-start | bytes 786436
Sparse Core Ops, SparseCore 0:
  18.3 89.5 all-gather.4
  109.5 81.6 all-gather.2
  339.6 167.4 reduce-scatter.2
  552.5 167.2 reduce-scatter.4

commit v2 on v1

--- a/solution.py
+++ b/solution.py
@@ -11,11 +11,11 @@
 EPS = 1e-6
 ROPE_BASE = 10000.0
 CHUNKS = 2
-GR = 16
-BG = 256
-BM = 384
+GR = 8
+BG = 320
+BM = 320
 TB = 128
-WIN = 64
+WIN = 32
 F32, BF = jnp.float32, jnp.bfloat16
 
 
@@ -34,15 +34,18 @@
 
     q, k, v = rope(q_ref[...]), rope(k_ref[...]), v_ref[...]
     n = q.shape[0] // qb
+    row = lax.broadcasted_iota(jnp.int32, (qb, qb), 0)
+    col = lax.broadcasted_iota(jnp.int32, (qb, qb), 1)
+    dims = (((1,), (1,)), ((), ()))
     for i in range(n):
+        qi = q[i * qb:(i + 1) * qb]
         kv = (i + 1) * qb
-        s = lax.dot_general(q[i * qb:(i + 1) * qb], k[:kv], (((1,), (1,)), ((), ())),
-                            preferred_element_type=F32) * scale
-        row = lax.broadcasted_iota(jnp.int32, (qb, kv), 0) + i * qb
-        col = lax.broadcasted_iota(jnp.int32, (qb, kv), 1)
-        s = jnp.where(row >= col, s, -jnp.inf)
-        p = jnp.exp(s - jnp.max(s, axis=-1, keepdims=True))
-        p = (p / jnp.sum(p, axis=-1, keepdims=True)).astype(BF)
+        diag = lax.dot_general(qi, k[i * qb:kv], dims, preferred_element_type=F32)
+        s = jnp.where(row >= col, diag, -jnp.inf)
+        if i:
+            s = jnp.concatenate([lax.dot_general(qi, k[:i * qb], dims, preferred_element_type=F32), s], axis=1)
+        p = jnp.exp((s - jnp.max(s, axis=-1, keepdims=True)) * scale)
+        p = (p * (1.0 / jnp.sum(p, axis=-1, keepdims=True))).astype(BF)
         o = jnp.dot(p, v[:kv], preferred_element_type=F32)
         o_ref[i * qb:(i + 1) * qb, :] = o.astype(BF)
 
@@ -63,58 +66,63 @@
     )(q, k, v, cos, sin)
 
 
-def _gather_kernel(ng, ge, gr0, gdst, stot, u_ref, rk_ref, x_hbm, xbuf, sem):
+def _gather_kernel(ge, gr0, gdst, stot, u_ref, rk_ref, x_hbm, xbuf, sem, used):
     s = pl.program_id(0)
     tc = u_ref.shape[0]
     per = BG // GR
-    total = stot[s]
     iota = lax.broadcasted_iota(jnp.int32, (GR, tc), 0)
 
-    def copies(m, act):
-        slot = lax.rem(m, 2)
+    @pl.when(s == 0)
+    def _():
+        used[0] = 0
+        for slot in range(2):
+            used[1 + 2 * slot] = 0
+            used[2 + 2 * slot] = 1 << 20
+
+    def copies(src, m, slot, act):
         for k in range(per):
             g = m * per + k
 
-            @pl.when(g < total)
+            @pl.when(g < stot[src])
             def _():
                 act(pltpu.make_async_copy(
                     xbuf.at[slot, pl.ds(k * GR, GR), :],
-                    x_hbm.at[pl.ds(pl.multiple_of(gdst[s, g] * GR, GR), GR), :],
+                    x_hbm.at[pl.ds(pl.multiple_of(gdst[src, g] * GR, GR), GR), :],
                     sem.at[slot, k]))
 
+    def drain(slot):
+        copies(used[1 + 2 * slot], used[2 + 2 * slot], slot, lambda c: c.wait())
+
     def tile(m, _):
-        @pl.when(m >= 2)
-        def _():
-            copies(m - 2, lambda c: c.wait())
-
+        slot = lax.rem(used[0], 2)
         parts = []
         for k in range(per):
             g = m * per + k
             row = rk_ref[0, pl.ds(ge[s, g], 1), :]
-            pos = iota + gr0[s, g]
-            parts.append((pos.astype(F32) == row).astype(F32).astype(BF))
-        onehot = jnp.concatenate(parts, axis=0)
-        xbuf[lax.rem(m, 2)] = jnp.dot(onehot, u_ref[...], preferred_element_type=F32).astype(BF)
-        copies(m, lambda c: c.start())
+            parts.append(((iota + gr0[s, g]).astype(F32) == row).astype(F32))
+        onehot = jnp.concatenate(parts, axis=0).astype(BF)
+        x = jnp.dot(onehot, u_ref[...], preferred_element_type=F32).astype(BF)
+        drain(slot)
+        xbuf[slot] = x
+        copies(s, m, slot, lambda c: c.start())
+        used[1 + 2 * slot] = s
+        used[2 + 2 * slot] = m
+        used[0] += 1
         return 0
 
-    tiles = lax.div(total + per - 1, per)
-    lax.fori_loop(0, tiles, tile, 0)
-
-    @pl.when(tiles >= 2)
-    def _():
-        copies(tiles - 2, lambda c: c.wait())
-
-    @pl.when(tiles >= 1)
-    def _():
-        copies(tiles - 1, lambda c: c.wait())
-
-
-def _gather(u, rk, tabs, rows, ng):
+    lax.fori_loop(0, lax.div(stot[s] + per - 1, per), tile, 0)
+
+    @pl.when(s == pl.num_programs(0) - 1)
+    def _():
+        drain(0)
+        drain(1)
+
+
+def _gather(u, rk, tabs, rows):
     srcs, el, tc = rk.shape
     d = u.shape[1]
     return pl.pallas_call(
-        functools.partial(_gather_kernel, ng),
+        _gather_kernel,
         out_shape=jax.ShapeDtypeStruct((rows, d), BF),
         grid_spec=pltpu.PrefetchScalarGridSpec(
             num_scalar_prefetch=4,
@@ -122,7 +130,8 @@
             in_specs=[pl.BlockSpec((tc, d), lambda s, *_: (s, 0)),
                       pl.BlockSpec((1, el, tc), lambda s, *_: (s, 0, 0))],
             out_specs=pl.BlockSpec(memory_space=pl.ANY),
-            scratch_shapes=[pltpu.VMEM((2, BG, d), BF), pltpu.SemaphoreType.DMA((2, BG // GR))],
+            scratch_shapes=[pltpu.VMEM((2, BG, d), BF), pltpu.SemaphoreType.DMA((2, BG // GR)),
+                            pltpu.SMEM((5,), jnp.int32)],
         ),
         compiler_params=pltpu.CompilerParams(vmem_limit_bytes=48 * 2**20),
         cost_estimate=pl.CostEstimate(flops=2 * rows * tc * d, bytes_accessed=4 * rows * d, transcendentals=0),
@@ -130,46 +139,77 @@
     )(*tabs, u, rk)
 
 
-def _expert_kernel(te, tv, nt, x_ref, w1_ref, w3_ref, w2_ref, y_ref):
-    i = pl.program_id(0)
-
-    @pl.when(i < nt[0])
-    def _():
-        x = x_ref[...]
+def _expert_kernel(tbase, tiles, tot, x_hbm, w1_ref, w3_ref, w2_ref, y_hbm, xbuf, ybuf, xsem, ysem):
+    e = pl.program_id(0)
+    last = pl.num_programs(0) - 1
+    nt = tbase[last] + tiles[last]
+    rows = lambda i: pl.ds(pl.multiple_of(i * BM, BM), BM)
+    load = lambda i: pltpu.make_async_copy(x_hbm.at[rows(i), :], xbuf.at[lax.rem(i, 2)], xsem.at[lax.rem(i, 2)])
+    save = lambda i: pltpu.make_async_copy(ybuf.at[lax.rem(i, 2)], y_hbm.at[rows(i), :], ysem.at[lax.rem(i, 2)])
+
+    @pl.when(e == 0)
+    def _():
+        load(0).start()
+
+    def tile(m, _):
+        i = tbase[e] + m
+        slot = lax.rem(i, 2)
+        load(i).wait()
+
+        @pl.when(i + 1 < nt)
+        def _():
+            load(i + 1).start()
+
+        x = xbuf[slot]
         h1 = jnp.dot(x, w1_ref[0], preferred_element_type=F32)
         h3 = jnp.dot(x, w3_ref[0], preferred_element_type=F32)
         hid = (jax.nn.silu(h1) * h3).astype(BF)
         y = jnp.dot(hid, w2_ref[0], preferred_element_type=F32)
-        row = lax.broadcasted_iota(jnp.int32, (y.shape[0], 1), 0)
-        y_ref[...] = jnp.where(row < tv[i], y, 0.0).astype(BF)
-
-
-def _experts(x, ue1, ue3, ue2, te, tv, nt, max_tiles):
+        row = lax.broadcasted_iota(jnp.int32, (BM, 1), 0)
+        y = jnp.where(row < tot[e] - m * BM, y, 0.0).astype(BF)
+
+        @pl.when(i >= 2)
+        def _():
+            save(i - 2).wait()
+
+        ybuf[slot] = y
+        save(i).start()
+        return 0
+
+    lax.fori_loop(0, tiles[e], tile, 0)
+
+    @pl.when(e == last)
+    def _():
+        @pl.when(nt >= 2)
+        def _():
+            save(nt - 2).wait()
+
+        save(nt - 1).wait()
+
+
+def _experts(x, ue1, ue3, ue2, tbase, tiles, tot, max_tiles):
     el, d, fe = ue1.shape
-
-    def rowmap(i, te, tv, nt):
-        return (jnp.minimum(i, nt[0] - 1), 0)
-
-    def wmap(i, te, tv, nt):
-        return (te[i], 0, 0)
-
     rows = max_tiles * BM
+    wmap = lambda e, *_: (e, 0, 0)
+    hbm = pl.BlockSpec(memory_space=pl.ANY)
     return pl.pallas_call(
         _expert_kernel,
         out_shape=jax.ShapeDtypeStruct((rows, d), BF),
         grid_spec=pltpu.PrefetchScalarGridSpec(
             num_scalar_prefetch=3,
-            grid=(max_tiles,),
-            in_specs=[pl.BlockSpec((BM, d), rowmap),
+            grid=(el,),
+            in_specs=[hbm,
                       pl.BlockSpec((1, d, fe), wmap),
                       pl.BlockSpec((1, d, fe), wmap),
                       pl.BlockSpec((1, fe, d), wmap)],
-            out_specs=pl.BlockSpec((BM, d), rowmap),
+            out_specs=hbm,
+            scratch_shapes=[pltpu.VMEM((2, BM, d), BF), pltpu.VMEM((2, BM, d), BF),
+                            pltpu.SemaphoreType.DMA((2,)), pltpu.SemaphoreType.DMA((2,))],
         ),
         compiler_params=pltpu.CompilerParams(vmem_limit_bytes=61 * 2**20),
         cost_estimate=pl.CostEstimate(flops=3 * rows * d * fe, bytes_accessed=6 * el * d * fe, transcendentals=rows * fe),
         name="experts",
-    )(te, tv, nt, x, ue1, ue3, ue2)
+    )(tbase, tiles, tot, x, ue1, ue3, ue2)
 
 
 def _combine_kernel(nb, st, tend, nwin, y_hbm, pos_ref, g_ref, o_ref, ybuf, sem):
@@ -250,6 +290,76 @@
         cost_estimate=pl.CostEstimate(flops=6 * srcs * tc * el * WIN * d, bytes_accessed=4 * srcs * tc * d, transcendentals=0),
         name="combine",
     )(st, tend, nwin, y, pos, gate)
+
+
+def _ffn_kernel(mb, z_ref, w1_ref, w3_ref, w2_ref, o_ref):
+    j = pl.program_id(0)
+    dims = (((1,), (1,)), ((), ()))
+
+    def rows(m, _):
+        at = pl.ds(pl.multiple_of(m * mb, mb), mb)
+        z = z_ref[at, :]
+        h1 = lax.dot_general(z, w1_ref[...], dims, preferred_element_type=F32)
+        h3 = lax.dot_general(z, w3_ref[...], dims, preferred_element_type=F32)
+        hid = (jax.nn.silu(h1) * h3).astype(BF)
+        y = jnp.dot(hid, w2_ref[...], preferred_element_type=F32)
+
+        @pl.when(j == 0)
+        def _():
+            o_ref[at, :] = y
+
+        @pl.when(j > 0)
+        def _():
+            o_ref[at, :] += y
+
+        return 0
+
+    lax.fori_loop(0, z_ref.shape[0] // mb, rows, 0)
+
+
+def _ffn(z, w1t, w3t, w2):
+    t, d = z.shape
+    ff = w2.shape[0]
+    ft = max(n for n in range(16, 1300, 16) if ff % n == 0)
+    one = pl.Buffered(1)
+    wblk = pl.BlockSpec((ft, d), lambda j: (j, 0))
+    return pl.pallas_call(
+        functools.partial(_ffn_kernel, min(t, 512)),
+        out_shape=jax.ShapeDtypeStruct((t, d), F32),
+        grid=(ff // ft,),
+        in_specs=[pl.BlockSpec((t, d), lambda j: (0, 0), pipeline_mode=one), wblk, wblk, wblk],
+        out_specs=pl.BlockSpec((t, d), lambda j: (0, 0), pipeline_mode=one),
+        compiler_params=pltpu.CompilerParams(vmem_limit_bytes=61 * 2**20),
+        cost_estimate=pl.CostEstimate(flops=6 * t * d * ff, bytes_accessed=6 * d * ff, transcendentals=t * ff),
+        name="ffn",
+    )(z, w1t, w3t, w2)
+
+
+def _final_kernel(per, a_ref, f_ref, *refs):
+    i = pl.program_id(0)
+    o_ref = refs[-1]
+    for c, m_ref in enumerate(refs[:-1]):
+        @pl.when(lax.div(i, per) == c)
+        def _():
+            o_ref[...] = (a_ref[...].astype(F32) + f_ref[...] + m_ref[...]).astype(BF)
+
+
+def _final(a, f, ms):
+    t, d = a.shape
+    rb = TB
+    per = ms[0].shape[0] // rb
+    blk = pl.BlockSpec((rb, d), lambda i: (i, 0))
+    mblk = [pl.BlockSpec((rb, d), lambda i, c=c: (jnp.clip(i - c * per, 0, per - 1), 0)) for c in range(len(ms))]
+    return pl.pallas_call(
+        functools.partial(_final_kernel, per),
+        out_shape=jax.ShapeDtypeStruct((t, d), BF),
+        grid=(t // rb,),
+        in_specs=[blk, blk] + mblk,
+        out_specs=blk,
+        compiler_params=pltpu.CompilerParams(vmem_limit_bytes=32 * 2**20),
+        cost_estimate=pl.CostEstimate(flops=2 * t * d, bytes_accessed=12 * t * d, transcendentals=0),
+        name="final_sum",
+    )(a, f, *ms)
 
 
 def _excl(x, axis):
@@ -279,18 +389,12 @@
     gr0 = jnp.where(live, gi[None, :] - jnp.sum(jnp.where(own, soff[:, None, :], 0), -1), 1 << 16) * GR
     gdst = jnp.sum(jnp.where(own, (seg - soff)[:, None, :], 0), -1) + gi[None, :]
     max_tiles = el * (-(-(srcs * (-(-cap // GR)) * GR) // BM))
-    nt = tiles.sum()
-    ti = jnp.arange(max_tiles, dtype=i32)
-    te = jnp.sum((ti[:, None] >= (tbase + tiles)[None, :]).astype(i32), -1)
-    te = jnp.minimum(te, el - 1)
-    mine = te[:, None] == eid[None, :]
-    tv = jnp.sum(jnp.where(mine, (tot * GR + tbase * BM)[None, :], 0), -1) - ti * BM
     tend = (tbase + tiles) * BM
     lo16 = lo // GR * GR
     st = (lo16 + seg[:, :, None] * GR).transpose(0, 2, 1).reshape(srcs * nb, el)
     nwin = jnp.max((hi - lo16 + WIN - 1) // WIN, axis=1).reshape(srcs * nb)
     pos = jnp.where(rk >= 0, rk.astype(i32) + seg[:, :, None] * GR, -1)
-    return (ge, gr0, gdst, stot), (te, tv, nt.reshape(1)), (st, tend, nwin), pos, max_tiles, ng
+    return (ge, gr0, gdst, stot), (tbase, tiles, tot * GR), (st, tend, nwin), pos, max_tiles
 
 
 def solution(mesh):
@@ -340,21 +444,18 @@
         for c in range(CHUNKS):
             rk = route[:, :el, c * tc:(c + 1) * tc]
             gt = route[:, el:, c * tc:(c + 1) * tc]
-            gtab, etab, ctab, ps, max_tiles, ng = _tables(rk, cap)
+            gtab, etab, ctab, ps, max_tiles = _tables(rk, cap)
             uc, gatekeeper = lax.optimization_barrier((us[c], gatekeeper))
-            xr = _gather(uc, rk, gtab, max_tiles * BM, ng)
+            xr = _gather(uc, rk, gtab, max_tiles * BM)
             y = _experts(xr, ue1, ue3, ue2, *etab, max_tiles)
             part = _combine(y, ps, gt, *ctab)
             part, gatekeeper = lax.optimization_barrier((part, gatekeeper))
             ms.append(lax.psum_scatter(part, 'ep', scatter_dimension=0, tiled=True))
-        m = jnp.concatenate(ms, axis=0)
 
         a = gatekeeper
         z = _rms(a, nf)
-        hid = (jax.nn.silu(jnp.dot(z, w1, preferred_element_type=F32)) * jnp.dot(z, w3, preferred_element_type=F32)).astype(BF)
-        af = a.astype(F32) + jnp.dot(hid, w2, preferred_element_type=F32)
-        af, m = lax.optimization_barrier((af, m))
-        return (af + m).astype(BF).reshape(b, s, d)
+        f = _ffn(z, w1.T, w3.T, w2)
+        return _final(a, f, ms).reshape(b, s, d)
 
     rows_spec = P(('dp', 'ep'))
     in_specs = (rows_spec,) * 3 + (P(),) * 11 + (P('ep'),) * 3

time: 770 us -> 717 us (0.931)
  matrix products: 233 us -> 55.1 us
  Pallas kernels: 462 us -> 590 us
  other arithmetic: 39.2 us -> 25.1 us
  local copies, waits for them, and re-layouts: 6.23 us -> 17.2 us
    dot_general x3 -> x0, matrix products: 181 us -> none  [the longest x1 65.2 us: local(): jnp.dot(z, w3, preferred_element_type=F32)]
    pallas_call x2 -> x4, Pallas kernels: 57.4 us -> 229 us  [the longest x1 170 us: _ffn(): pl.pallas_call(functools.partial(_ffn_kernel, min(t, 512)), out_shape=jax...]
    pallas_call x2, Pallas kernels: 262 us -> 236 us  [_experts(): pl.pallas_call(_expert_kernel, out_shape=jax.ShapeDtypeStruct((rows, d),...]
    pallas_call x2, Pallas kernels: 102 us -> 85.4 us  [_combine(): pl.pallas_call(functools.partial(_combine_kernel, nb), out_shape=jax.Shap...]
    unnamed x51 -> x45, local copies, waits for them, and re-layouts: 3.23 us -> 14 us
    reshape x1 -> x0, other arithmetic: 9.37 us -> none  [local(): return (af + m).astype(BF).reshape(b, s, d)]
    concatenate x1 -> x0, other arithmetic: 7.94 us -> none  [local(): m = jnp.concatenate(ms, axis=0)]
  transfers between devices with their start and end apart: 5 -> 5, of which waited for: 0 -> 0; matrix products, arithmetic and copies ran while one was open for 33% -> 10% of each run, Pallas kernels for 61% -> 83%
where the time goes in v2:
time: 717 us; the launch traced here: 708 us
  Pallas kernels  590 us (82%)
  matrix products  55.1 us (8%)
  other arithmetic  25.1 us (4%)
  local copies, waits for them, and re-layouts  17.2 us (2%)
  between operations  13.9 us (2%)
    pallas_call x2, Pallas kernels, _experts(): pl.pallas_call(_expert_kernel, out_shape=jax.ShapeDtypeStruct((rows, d),...  236 us
    pallas_call x1, Pallas kernels, _ffn(): pl.pallas_call(functools.partial(_ffn_kernel, min(t, 512)), out_shape=jax...  170 us
    pallas_call x2, Pallas kernels, _combine(): pl.pallas_call(functools.partial(_combine_kernel, nb), out_shape=jax.Shap...  85.4 us
    pallas_call x2, Pallas kernels, _gather(): pl.pallas_call(_gather_kernel, out_shape=jax.ShapeDtypeStruct((rows, d),...  55.1 us
    pallas_call x1, Pallas kernels, _attention(): pl.pallas_call(functools.partial(_attn_kernel, HEAD ** (-0.5), min(256, s...  40 us
  transfers between devices with their start and end apart: 5, of which 0 were waited for; matrix products, arithmetic and copies ran while one was open for 10% of the time, Pallas kernels for 83%

profile of v2, /device:TPU:112, one launch (start us, length us, event | category | flops | bytes accessed | tf_op | source)
XLA Modules:
  0.0 707.6 jit_solution(7196847385543547374)
XLA Ops:
  6.6 3.1 fusion.7
  9.7 0.7 convert_element_type.83
  10.4 3.2 fusion.2
  13.6 2.0 copy-done.7
  15.6 2.6 fusion.76
  18.3 0.1 all-gather.3.cloned.1.call-start
  18.4 0.7 all-gather.3.cloned.1.call-update
  19.2 0.2 fusion.9
  19.4 0.1 reshape.348
  19.4 0.2 fusion.10
  19.7 0.1 reshape.349
  19.8 3.6 select_reduce_fusion
  23.4 0.1 fusion.11
  23.5 0.1 divide_bitcast_fusion
  23.6 0.9 pad_maximum_fusion
  24.5 5.3 all-to-all-start
  29.8 0.1 reduce-scatter.3.cloned.1.call-start
  29.9 1.9 fusion.12
  31.8 0.3 pad_maximum_fusion.1
  32.2 14.1 %convolution_convert_fusion.v_ref = bf16[1024,2048]{1,0:T(8,128)(2,1)S(1)} fusion(bf16[2048,2048]{1,0:T(8,128)(2,1)} %param.22, bf16[1,1024,2048]{2,1,0:T(8,128)(2,1)} %param.17, f32[2048]{0:T(1024)S(1)} %convert_element_type.89, f32[1024]{0:T(1024)S(1)} %add_rsqrt_fusion.1), kind=kOutput, calls=%fused_computation.14 | convolution fusion | flops 8600420352 | bytes 16789504 | tf_op jit(solution)/shard_map/dot_general | solution.py:437
  46.3 11.2 %fusion.68.k_ref = f32[1024,2048]{1,0:T(8,128)} fusion(bf16[2048,2048]{1,0:T(8,128)(2,1)S(1)} %bitcast.137, bf16[1,1024,2048]{2,1,0:T(8,128)(2,1)S(1)} %copy-done.8, f32[2048]{0:T(1024)S(1)} %convert_element_type.89, f32[1024]{0:T(1024)S(1)} %add_rsqrt_fusion.1), kind=kOutput, calls=%fused_computation.188 | convolution fusion | flops 8598323200 | bytes 20983808 | tf_op jit(solution)/shard_map/dot_general | solution.py:436
  57.5 13.2 %fusion.70.q_ref = f32[1024,2048]{1,0:T(8,128)} fusion(bf16[2048,2048]{1,0:T(8,128)(2,1)} %param.20, bf16[1,1024,2048]{2,1,0:T(8,128)(2,1)S(1)} %copy-done.8, f32[2048]{0:T(1024)S(1)} %convert_element_type.89, f32[1024]{0:T(1024)S(1)} %add_rsqrt_fusion.1), kind=kOutput, calls=%fused_computation.189 | convolution fusion | flops 8598323200 | bytes 20983808 | tf_op jit(solution)/shard_map/dot_general | solution.py:435
  70.8 40.0 %attention.1 = bf16[1024,2048]{1,0:T(8,128)(2,1)S(1)} custom-call(f32[1024,2048]{1,0:T(8,128)} %fusion.70.q_ref, f32[1024,2048]{1,0:T(8,128)} %fusion.68.k_ref, bf16[1024,2048]{1,0:T(8,128)(2,1)S(1)} %convolution_convert_fusion.v_ref, f32[1024,128]{1,0:T(8,128)S(1)} %get-tuple-element.76.cos_ref, f32[1024,128]{1,0:T(8,128)S(1)} %get-tuple-element.77.sin_ref), custom_call_target="tpu_custom_call" | custom-call | flops 8589934592 | bytes 25165824 | tf_op jit(solution)/shard_map/attention/pallas_call | solution.py:57
  110.8 12.7 %fusion.8.a_ref = bf16[1024,2048]{1,0:T(8,128)(2,1)} fusion(bf16[1,1024,2048]{2,1,0:T(8,128)(2,1)S(1)} %copy-done.8, bf16[1024,2048]{1,0:T(8,128)(2,1)S(1)} %attention.1, bf16[2048,2048]{1,0:T(8,128)(2,1)} %param.23), kind=kOutput, calls=%fused_computation.13 | convolution fusion | flops 8596226048 | bytes 20971520 | tf_op jit(solution)/shard_map/dot_general | solution.py:440
  123.5 1.2 bitcast_reduce_fusion
  124.6 0.3 fusion.32
  125.0 0.1 fusion.72
  125.1 0.2 reduce_window_sum.71
  125.3 0.1 copy.40
  125.4 0.1 reshape.356.nwin
  125.5 0.2 reduce-window.15
  125.7 0.9 fusion.23
  126.6 0.7 fusion.73
  127.3 0.2 reduce-window.14
  127.5 0.4 copy-done.9
  127.9 0.6 broadcast_multiply_fusion
  128.5 0.6 broadcast_multiply_fusion.1
  129.0 0.5 copy-done.16
  129.6 0.6 fusion.17
  130.2 0.1 select_reduce_fusion.1
  130.3 0.1 iota_add_fusion
  130.4 0.1 add_select_fusion
  130.6 27.4 %gather_rows.2.x_hbm = bf16[12800,2048]{1,0:T(8,128)(2,1)} custom-call(s32[8,232]{1,0:T(8,128)S(1)} %get-tuple-element.25.ge, s32[8,232]{1,0:T(8,128)S(1)} %get-tuple-element.75.gr0, s32[8,232]{1,0:T(8,128)S(1)} %get-tuple-element.74.gdst, s32[8]{0:T(128)S(1)} %get-tuple-element.29.stot, bf16[4096,2048]{1,0:T(8,128)(2,1)} %all-gather.5.cloned.1.call-done.u_ref, ...), custom_call_target="tpu_custom_call" | custom-call | flops 26843545600 | bytes 104857600 | tf_op jit(solution)/shard_map/gather_rows/pallas_call | solution.py:124
  158.0 118.0 %experts.2.y_hbm = bf16[12800,2048]{1,0:T(8,128)(2,1)} custom-call(s32[8]{0:T(128)} %get-tuple-element.36.tbase, s32[8]{0:T(128)} %get-tuple-element.37.tiles, s32[8]{0:T(128)} %get-tuple-element.60.tot, bf16[12800,2048]{1,0:T(8,128)(2,1)} %gather_rows.2.x_hbm, bf16[8,2048,1408]{2,1,0:T(8,128)(2,1)} %w1_ref.3, bf16[8,2048,1408]{2,1,0:T(8,128)(2,1)} %w3_ref.3, ...), custom_call_target="tpu_custom_call" | custom-call | flops 110729625600 | bytes 138412032 | tf_op jit(solution)/shard_map/experts/pallas_call | solution.py:195
  276.0 43.6 %combine.2 = f32[4096,2048]{1,0:T(8,128)} custom-call(s32[32,8]{1,0:T(8,128)S(1)} %bitcast.131, s32[8]{0:T(128)S(1)} %get-tuple-element.61.tend, s32[32]{0:T(128)S(1)} %reshape.356.nwin, bf16[12800,2048]{1,0:T(8,128)(2,1)} %experts.2.y_hbm, s32[8,8,512]{2,1,0:T(8,128)S(1)} %get-tuple-element.56.pos_ref, f32[8,8,512]{2,1,0:T(8,128)S(1)} %get-tuple-element.52.g_ref), custom_call_target="tpu_custom_call" | custom-call | flops 12884901888 | bytes 33554432 | tf_op jit(solution)/shard_map/combine/pallas_call | solution.py:279
  319.8 0.1 reduce-scatter.5.cloned.1.call-start
  319.9 0.5 copy-done.10
  320.4 0.2 reduce_window_sum.67
  320.5 0.1 copy.36
  320.6 0.1 reshape.353.nwin
  320.7 0.1 select_reduce_fusion.4
  320.9 0.1 iota_add_fusion.1
  320.9 27.7 %gather_rows.3.x_hbm = bf16[12800,2048]{1,0:T(8,128)(2,1)} custom-call(s32[8,232]{1,0:T(8,128)S(1)} %get-tuple-element.28.ge, s32[8,232]{1,0:T(8,128)S(1)} %get-tuple-element.73.gr0, s32[8,232]{1,0:T(8,128)S(1)} %get-tuple-element.72.gdst, s32[8]{0:T(128)S(1)} %copy-done.6, bf16[4096,2048]{1,0:T(8,128)(2,1)} %all-gather.3.cloned.1.call-done.u_ref, ...), custom_call_target="tpu_custom_call" | custom-call | flops 26843545600 | bytes 104857600 | tf_op jit(solution)/shard_map/gather_rows/pallas_call | solution.py:124
  348.6 118.0 %experts.3.y_hbm = bf16[12800,2048]{1,0:T(8,128)(2,1)} custom-call(s32[8]{0:T(128)} %get-tuple-element.44.tbase, s32[8]{0:T(128)} %get-tuple-element.45.tiles, s32[8]{0:T(128)} %get-tuple-element.62.tot, bf16[12800,2048]{1,0:T(8,128)(2,1)} %gather_rows.3.x_hbm, bf16[8,2048,1408]{2,1,0:T(8,128)(2,1)} %w1_ref.3, bf16[8,2048,1408]{2,1,0:T(8,128)(2,1)} %w3_ref.3, ...), custom_call_target="tpu_custom_call" | custom-call | flops 110729625600 | bytes 138412032 | tf_op jit(solution)/shard_map/experts/pallas_call | solution.py:195
  466.6 41.7 %combine.3 = f32[4096,2048]{1,0:T(8,128)} custom-call(s32[32,8]{1,0:T(8,128)S(1)} %bitcast.132, s32[8]{0:T(128)S(1)} %get-tuple-element.63.tend, s32[32]{0:T(128)S(1)} %reshape.353.nwin, bf16[12800,2048]{1,0:T(8,128)(2,1)} %experts.3.y_hbm, s32[8,8,512]{2,1,0:T(8,128)S(1)} %get-tuple-element.55.pos_ref, f32[8,8,512]{2,1,0:T(8,128)S(1)} %get-tuple-element.51.g_ref), custom_call_target="tpu_custom_call" | custom-call | flops 12884901888 | bytes 33554432 | tf_op jit(solution)/shard_map/combine/pallas_call | solution.py:279
  508.4 0.6 copy-done.19
  509.1 3.1 fusion.4
  512.2 5.2 fusion.6.z_ref
  517.3 169.7 %ffn.1.f_ref = f32[1024,2048]{1,0:T(8,128)} custom-call(bf16[1024,2048]{1,0:T(8,128)(2,1)} %fusion.6.z_ref, bf16[10944,2048]{1,0:T(8,128)(2,1)} %bitcast.134, bf16[10944,2048]{1,0:T(8,128)(2,1)} %bitcast.135, bf16[10944,2048]{1,0:T(8,128)(2,1)} %w2_ref.5), custom_call_target="tpu_custom_call" | custom-call | flops 137707388928 | bytes 134479872 | tf_op jit(solution)/shard_map/ffn/pallas_call | solution.py:326
  687.0 2.2 copy-done.2
  689.2 3.4 copy-done.3
  692.6 2.2 copy-done.4
  694.8 2.2 copy-done.5
  697.0 3.8 final_sum.1
  (64 shorter events, 0.5 us)
Async XLA Ops:
  6.5 13.2 %copy-start = (bf16[2048,64]{0,1:T(8,128)(2,1)S(1)}, bf16[2048,64]{0,1:T(8,128)(2,1)}, u32[]{:S(2)}) copy-start(bf16[2048,64]{0,1:T(8,128)(2,1)} %param.29) | copy-start | bytes 786436
  6.6 124.0 %all-gather.5.cloned.1.call-start = ((), (), s32[]{:S(2)}) async-start(), calls=%async_computation.4 | async-start | bytes 18874368 | tf_op jit(solution)/shard_map/all_gather | solution.py:414
  13.6 2.0 copy-start.7
  15.6 3.5 copy-start.14
  18.3 11.6 %copy-start.18 = (bf16[2048]{0:T(1024)(128)(2,1)S(1)}, bf16[2048]{0:T(1024)(128)(2,1)}, u32[]{:S(2)}) copy-start(bf16[2048]{0:T(1024)(128)(2,1)} %param.19) | copy-start | bytes 12292
  18.3 302.6 %all-gather.3.cloned.1.call-start = ((), (), s32[]{:S(2)}) async-start(), calls=%async_computation.3 | async-start | bytes 18874368 | tf_op jit(solution)/shard_map/all_gather | solution.py:414
  24.5 99.0 %all-to-all-start = ((f32[8,16,1024]{2,1,0:T(8,128)}), f32[8,16,1024]{2,1,0:T(8,128)S(1)}, u32[]{:S(2)}, u32[]{:S(2)}) async-start(f32[8,16,1024]{2,1,0:T(8,128)} %pad_maximum_fusion), calls=%async_computation | async-start | bytes 1048576 | tf_op jit(solution)/shard_map/all_to_all | solution.py:426
  29.8 657.3 %reduce-scatter.3.cloned.1.call-start = ((), (), s32[]{:S(2)}) async-start(), calls=%async_computation.5 | async-start | bytes 37748736 | tf_op jit(solution)/shard_map/reduce_scatter | solution.py:453
  31.8 14.5 %slice-start = ((s8[8388608]{0:T(1024)(128)(4,1)}), s8[4194304]{0:T(1024)(128)(4,1)S(1)}, s32[]{:S(2)}) async-start(s8[8388608]{0:T(1024)(128)(4,1)} %bitcast.136), calls=%async_computation.7 | async-start | bytes 8388608
  32.1 14.1 %copy-start.8 = (bf16[1,1024,2048]{2,1,0:T(8,128)(2,1)S(1)}, bf16[1,1024,2048]{2,1,0:T(8,128)(2,1)}, u32[]{:S(2)}) copy-start(bf16[1,1024,2048]{2,1,0:T(8,128)(2,1)} %param.17) | copy-start | bytes 12582916
  32.1 14.1 %slice-start.1 = ((s8[8388608]{0:T(1024)(128)(4,1)}), s8[4194304]{0:T(1024)(128)(4,1)S(1)}, s32[]{:S(2)}) async-start(s8[8388608]{0:T(1024)(128)(4,1)} %bitcast.136), calls=%async_computation.8 | async-start | bytes 8388608
  127.3 0.6 copy-start.9
  127.9 1.2 copy-start.12
  129.0 0.5 copy-start.16
  319.7 0.7 copy-start.10
  319.7 0.8 copy-start.15
  319.7 1.0 copy-start.11
  319.7 1.0 copy-start.13
  319.7 1.0 copy-start.17
  319.7 1.1 copy-start.6
  319.8 367.2 %reduce-scatter.5.cloned.1.call-start = ((), (), s32[]{:S(2)}) async-start(), calls=%async_computation.6 | async-start | bytes 37748736 | tf_op jit(solution)/shard_map/reduce_scatter | solution.py:453
  508.4 0.7 copy-start.19
  517.3 183.5 %copy-start.1 = (bf16[2048,64]{0,1:T(8,128)(2,1)S(1)}, bf16[2048,64]{0,1:T(8,128)(2,1)}, u32[]{:S(2)}) copy-start(bf16[2048,64]{0,1:T(8,128)(2,1)} %param.29) | copy-start | bytes 786436
  687.0 2.2 copy-start.2
  689.2 3.4 copy-start.3
  692.6 2.2 copy-start.4
  694.8 2.2 copy-start.5
Sparse Core Ops, SparseCore 0:
  18.4 89.5 all-gather.4
  109.6 81.6 all-gather.2
  319.9 179.0 reduce-scatter.2
  508.6 177.4 reduce-scatter.4
